TPU v7x, 32 devices: a whole 2x2x4 slice. The times are simulated.
32 devices in a mesh: dp: 4 (over x, core), section: 2 (over y), expert: 4 (over z).
Axes of the slice: x: 2, y: 2, z: 4, core: 2. Of those that a mesh axis runs over, the one named last changes fastest.
Arguments:
- paths_in: bfloat16 [2, 256, 4, 7168], P(None, 'expert', None, 'dp'), may hold values from -12 to 12
- path_proj: bfloat16 [2, 24, 4, 7168], P('section', None, None, 'dp'), may hold values from -0.03125 to 0.03125
- coef_bias: float32 [2, 24], P('section'), may hold values from -4 to 4
- norm_gain: bfloat16 [2, 7168], P('section', 'dp'), may hold values from 0.25 to 1.75
- w_gate_up: bfloat16 [2, 4, 7168, 2, 512], P('section', 'expert', 'dp'), may hold values from -0.0625 to 0.0625
- w_down: bfloat16 [2, 4, 512, 7168], P('section', 'expert', None, 'dp'), may hold values from -0.1875 to 0.1875
- routes: int32 [2, 2, 256, 1], P('section', None, 'expert'), may hold values from 0 to 1; in each aligned block of 64 rows (0 to 63, 64 to 127, ..., all dimensions but the last counted through in order) at most 32 rows name the same one
- route_gate: float32 [2, 2, 256, 1], P('section', None, 'expert'), may hold values from 0.2 to 1
Outputs:
- paths_out: bfloat16 [2, 2, 256, 4, 7168], P('section', None, 'expert', None, 'dp')
Inputs may be any that keep to these rules, and one draw needn't show every extreme that they name: `routes`: each row names exactly one expert. In each aligned block of 64 rows (the tokens of one index of expert in one layer and micro-batch) no expert is named more than 32 times, a bound that some block reaches.
All inputs are finite; a program needn't handle non-finite values.
Results may differ from a plain program's by a relative error of at most 0.014.
Values may be sent and summed in bfloat16 or wider, within the bound.
A program may use at most 64 MiB of HBM per device.

v0:
```python
import jax
import jax.numpy as jnp
from jax import lax
from jax.sharding import PartitionSpec as P

D = 7168
RESIDUAL_STREAMS = 4
SINK = 20
EPSILON = 1e-06


def passed_along(value, axis, steps):
    count = lax.axis_size(axis)
    leading, last = (max(0, -steps), min(count, count - steps))
    return lax.ppermute(value, axis, [(source, source + steps) for source in range(leading, last)])


def doubly_stochastic_project(stream_mixer):
    for repeat in range(SINK):
        stream_mixer = stream_mixer / jnp.sum(stream_mixer, axis=2, keepdims=True)
        stream_mixer = stream_mixer / jnp.sum(stream_mixer, axis=1, keepdims=True)
    return stream_mixer


def expert_block(received, gate_up, down_proj):
    sources, items, width = received.shape
    slot_rows = received.reshape(sources * items, width)
    inner = down_proj.shape[0]
    hidden_pre = jnp.dot(slot_rows, gate_up, preferred_element_type=jnp.float32)
    summed = lax.psum(hidden_pre, "dp")
    hidden = (jax.nn.silu(summed[:, :inner]) * summed[:, inner:]).astype(jnp.bfloat16)
    expert_output_rows = jnp.dot(hidden, down_proj, preferred_element_type=jnp.float32)
    expert_output_rows = expert_output_rows.astype(jnp.bfloat16).reshape(sources, items, width)
    return lax.all_to_all(expert_output_rows, "expert", split_axis=0, concat_axis=0, tiled=True)


def mix_layer(residual, path_proj, coef_bias, norm_gain, gate_up, down_proj, routes_now, gates_now):
    rows, paths, width = residual.shape
    widened = residual.astype(jnp.float32)
    square_part = jnp.sum(widened * widened, axis=(1, 2))
    projected = jnp.einsum("tsd,csd->tc", residual, path_proj, preferred_element_type=jnp.float32)
    path_gram = jnp.einsum("tid,tjd->tij", residual, residual, preferred_element_type=jnp.float32)
    square_sum, projected, path_gram = lax.psum((square_part, projected, path_gram), "dp")
    router_scores = (
        projected * lax.rsqrt(square_sum / (RESIDUAL_STREAMS * D) + EPSILON)[:, None]
        + coef_bias[None, :]
    )
    pre_weight = jax.nn.sigmoid(router_scores[:, :RESIDUAL_STREAMS])
    post_weight = 2.0 * jax.nn.sigmoid(router_scores[:, RESIDUAL_STREAMS : 2 * RESIDUAL_STREAMS])
    stream_mixer = doubly_stochastic_project(
        jnp.exp(router_scores[:, 2 * RESIDUAL_STREAMS :]).reshape(
            -1, RESIDUAL_STREAMS, RESIDUAL_STREAMS
        )
    )
    merged = jnp.sum(pre_weight[:, :, None] * widened, axis=1)
    width_sum = jnp.einsum(
        "ti,tij,tj->t", pre_weight, path_gram, pre_weight, precision=lax.Precision.HIGHEST
    )
    normed = (
        merged
        * lax.rsqrt(width_sum / D + EPSILON)[:, None]
        * norm_gain.astype(jnp.float32)[None, :]
    ).astype(jnp.bfloat16)
    expert_count = lax.axis_size("expert") // 2
    selected_expert_count = routes_now.shape[1]
    capacity = min(rows, max(2, (rows * selected_expert_count + expert_count - 1) // expert_count))
    slot_count = expert_count * capacity
    flat_routes = routes_now.reshape(-1)
    chosen = (flat_routes[:, None] == jnp.arange(expert_count, dtype=jnp.int32)[None, :]).astype(
        jnp.int32
    )
    earlier = jnp.cumsum(chosen, axis=0) - chosen
    rank_within = jnp.sum(earlier * chosen, axis=1)
    slot_of = flat_routes * capacity + rank_within
    slot_match = jnp.arange(slot_count, dtype=jnp.int32)[:, None] == slot_of[None, :]
    dispatch_map = jnp.sum(
        slot_match.reshape(slot_count, rows, selected_expert_count).astype(jnp.int32), axis=2
    ).astype(jnp.bfloat16)
    gate_spread = jnp.where(slot_match, gates_now.reshape(-1)[None, :], 0.0)
    combine_map = jnp.sum(gate_spread.reshape(slot_count, rows, selected_expert_count), axis=2).T
    outgoing = jnp.dot(dispatch_map, normed, preferred_element_type=jnp.float32).astype(
        jnp.bfloat16
    )
    outgoing = outgoing.reshape(expert_count, 1, capacity, width)
    outgoing = jnp.broadcast_to(outgoing, (expert_count, 2, capacity, width)).reshape(
        2 * expert_count, capacity, width
    )
    returned = expert_block(
        lax.all_to_all(outgoing, "expert", split_axis=0, concat_axis=0, tiled=True),
        gate_up=gate_up,
        down_proj=down_proj,
    )
    halves = returned.reshape(expert_count, 2, capacity, width).astype(jnp.float32)
    expert_weighted_total = halves[:, 0] + halves[:, 1]
    branch = jnp.dot(
        combine_map,
        expert_weighted_total.reshape(slot_count, width),
        precision=lax.Precision.HIGHEST,
    )
    carried = jnp.einsum("tji,tid->tjd", stream_mixer, widened, precision=lax.Precision.HIGHEST)
    return (carried + post_weight[:, :, None] * branch[:, None, :]).astype(jnp.bfloat16)


def body(paths_in, path_proj, coef_bias, norm_gain, w_gate_up, w_down, routes, route_gate):
    section_index = lax.axis_index("section")
    section_count = lax.axis_size("section")
    micro_count = paths_in.shape[0]
    gate_up = w_gate_up[0, 0].reshape(w_gate_up.shape[2], -1)
    down_proj = w_down[0, 0]
    incoming = jnp.zeros(paths_in.shape[1:], jnp.bfloat16)
    results = jnp.zeros(paths_in.shape, jnp.bfloat16)
    slot_index = jnp.arange(micro_count, dtype=jnp.int32)
    total_steps = micro_count + section_count - 1
    for time_step in range(total_steps):
        micro_index = time_step - section_index
        clipped = jnp.clip(micro_index, 0, micro_count - 1)
        entering = lax.dynamic_index_in_dim(paths_in, clipped, 0, keepdims=False)
        current = jnp.where(section_index == 0, entering, incoming)
        routes_now = lax.dynamic_index_in_dim(routes[0], clipped, 0, keepdims=False)
        gates_now = lax.dynamic_index_in_dim(route_gate[0], clipped, 0, keepdims=False)
        leaving = mix_layer(
            current,
            path_proj[0],
            coef_bias[0],
            norm_gain[0],
            gate_up,
            down_proj,
            routes_now,
            gates_now,
        )
        results = jnp.where(
            (slot_index == micro_index)[:, None, None, None], leaving[None], results
        )
        if time_step + 1 < total_steps:
            incoming = passed_along(leaving, "section", 1)
    return results[None]


def solution(mesh):
    in_specs = (
        P(None, "expert", None, "dp"),
        P("section", None, None, "dp"),
        P("section", None),
        P("section", "dp"),
        P("section", "expert", "dp", None, None),
        P("section", "expert", None, "dp"),
        P("section", None, "expert", None),
        P("section", None, "expert", None),
    )
    out_specs = P("section", None, "expert", None, "dp")
    return jax.shard_map(body, mesh=mesh, in_specs=in_specs, out_specs=out_specs, check_vma=False)
```

profile of v0, /device:TPU:0, one launch (start us, length us, event | category | flops | bytes accessed | tf_op | source)
XLA Modules:
  0.0 375.9 jit_solution(183301139221659460)
XLA Ops:
  6.5 1.6 constant_dynamic-slice_fusion.6
  8.6 1.2 fusion.129
  10.1 15.1 %all-reduce.2 = (f32[64,24]{0,1:T(8,128)S(1)}, f32[64]{0:T(128)S(1)}, f32[64,4,4]{2,1,0:T(4,128)}) all-reduce(f32[64,24]{0,1:T(8,128)S(1)} %convolution_bitcast_fusion.2, f32[64]{0:T(128)S(1)} %get-tuple-element.18, f32[64,4,4]{2,1,0:T(4,128)S(1)} %fusion.129), channel_id=1, replica_groups=mesh['dp'=4,'section'=2,'expert'=4] {'dp'}, use_global_device_ids=true, to_apply=%region_0.1 | all-reduce | flops 2624 | bytes 20992 | tf_op jit(solution)/shard_map/psum | solution.py:43
  27.2 1.0 fusion.61
  28.2 1.4 copy.290
  29.6 1.5 fusion.265
  31.1 0.9 multiply_reduce_fusion.2
  32.5 1.3 fusion.203
  35.0 1.4 reduce_window_sum.20
  36.4 0.9 select_reduce_fusion.2
  38.8 0.9 convolution_convert_fusion.5
  40.5 4.9 %all-to-all-start = ((bf16[4,32,1792]{2,1,0:T(8,128)(2,1)}), bf16[4,32,1792]{2,1,0:T(8,128)(2,1)S(1)}, u32[]{:S(2)}, u32[]{:S(2)}) async-start(bf16[4,32,1792]{2,1,0:T(8,128)(2,1)} %bitcast.125), calls=%async_computation | async-start | bytes 917504 | tf_op jit(solution)/shard_map/all_to_all | solution.py:89
  45.4 1.3 slice_exponential_fusion.2
  46.7 1.3 reduce_sum.1186
  56.0 0.8 divide_reduce_fusion.50
  58.4 4.8 %copy.306 = bf16[224,8,2,512]{3,1,2,0:T(8,128)(2,1)} copy(bf16[224,8,2,512]{3,2,1,0:T(2,128)(2,1)} %bitcast.121) | data formatting | bytes 7340032
  63.3 1.2 divide_reduce_fusion.45
  64.5 3.5 fusion.266
  68.0 0.8 divide_reduce_fusion.44
  68.9 2.0 divide_reduce_fusion.43
  70.8 31.3 %all-reduce.7.cloned.1.call-done = f32[128,1024]{1,0:T(8,128)} async-done(((f32[128,1024]{1,0:T(8,128)}), f32[128,1024]{1,0:T(8,128)}) %all-reduce.7.cloned.1.call-update) | async-done | bytes 524304 | tf_op jit(solution)/shard_map/psum | solution.py:30
  102.2 2.2 convolution_convert_fusion.2
  104.4 4.6 %all-to-all-start.1 = ((bf16[4,32,1792]{2,1,0:T(8,128)(2,1)}), bf16[4,32,1792]{2,1,0:T(8,128)(2,1)S(1)}, u32[]{:S(2)}, u32[]{:S(2)}) async-start(bf16[4,32,1792]{2,1,0:T(8,128)(2,1)} %bitcast.139), calls=%async_computation.1 | async-start | bytes 917504 | tf_op jit(solution)/shard_map/all_to_all | solution.py:34
  110.6 1.3 multiply_divide_fusion.5
  111.9 1.4 copy.275
  113.4 1.4 copy.277
  114.7 1.3 fusion.199
  116.1 5.1 %all-to-all-done.1 = bf16[4,32,1792]{2,1,0:T(8,128)(2,1)S(1)} async-done(((bf16[4,32,1792]{2,1,0:T(8,128)(2,1)}), bf16[4,32,1792]{2,1,0:T(8,128)(2,1)S(1)}, u32[]{:S(2)}, u32[]{:S(2)}) %all-to-all-start.1) | async-done | bytes 458784 | tf_op jit(solution)/shard_map/all_to_all | solution.py:34
  122.4 3.2 fusion.57
  125.6 4.3 %collective-permute-start = (bf16[64,4,1792]{2,1,0:T(4,128)(2,1)}, bf16[64,4,1792]{2,1,0:T(4,128)(2,1)}, u32[]{:S(2)}, u32[]{:S(2)}) collective-permute-start(bf16[64,4,1792]{2,1,0:T(4,128)(2,1)} %fusion.57), channel_id=1, source_target_pairs={{0,4},{1,5},{2,6},{3,7},{8,12},{9,13},{10,14},{11,15},{16,20},{17,... | collective-permute-start | bytes 2752520 | tf_op jit(solution)/shard_map/ppermute | solution.py:15
  130.9 17.1 %collective-permute-done = bf16[64,4,1792]{2,1,0:T(4,128)(2,1)} collective-permute-done((bf16[64,4,1792]{2,1,0:T(4,128)(2,1)}, bf16[64,4,1792]{2,1,0:T(4,128)(2,1)}, u32[]{:S(2)}, u32[]{:S(2)}) %collective-permute-start) | collective-permute-done | bytes 917536 | tf_op jit(solution)/shard_map/ppermute | solution.py:15
  148.0 2.6 fusion.62
  150.6 1.1 fusion.267
  152.1 11.8 %all-reduce.1 = (f32[64,24]{0,1:T(8,128)S(1)}, f32[64]{0:T(128)S(1)}, f32[64,4,4]{2,1,0:T(4,128)S(1)}) all-reduce(f32[64,24]{0,1:T(8,128)S(1)} %convolution_bitcast_fusion.1, f32[64]{0:T(128)S(1)} %get-tuple-element.16, f32[64,4,4]{2,1,0:T(4,128)S(1)} %fusion.267), channel_id=1, replica_groups=mesh['dp'=4,'section'=2,'expert'=4] {'dp'}, use_global_device_ids=true, to_apply=%region_48.49 | all-reduce | flops 2624 | bytes 20992 | tf_op jit(solution)/shard_map/psum | solution.py:43
  165.4 1.3 fusion.63
  168.5 3.5 all-to-all-start.2
  172.0 1.3 reduce_sum.1229
  184.6 1.2 divide_reduce_fusion.27
  185.8 3.5 fusion.269
  189.3 0.8 divide_reduce_fusion.26
  190.1 2.0 divide_reduce_fusion.25
  192.1 33.4 %all-reduce.9.cloned.1.call-done = f32[128,1024]{1,0:T(8,128)} async-done(((f32[128,1024]{1,0:T(8,128)}), f32[128,1024]{1,0:T(8,128)}) %all-reduce.9.cloned.1.call-update) | async-done | bytes 524304 | tf_op jit(solution)/shard_map/psum | solution.py:30
  225.6 2.2 convolution_convert_fusion.1
  227.8 4.6 %all-to-all-start.3 = ((bf16[4,32,1792]{2,1,0:T(8,128)(2,1)}), bf16[4,32,1792]{2,1,0:T(8,128)(2,1)S(1)}, u32[]{:S(2)}, u32[]{:S(2)}) async-start(bf16[4,32,1792]{2,1,0:T(8,128)(2,1)} %bitcast.137), calls=%async_computation.3 | async-start | bytes 917504 | tf_op jit(solution)/shard_map/all_to_all | solution.py:34
  234.8 1.3 multiply_divide_fusion.4
  236.1 1.5 copy.282
  237.6 1.4 copy.283
  239.0 5.6 %all-to-all-done.3 = bf16[4,32,1792]{2,1,0:T(8,128)(2,1)S(1)} async-done(((bf16[4,32,1792]{2,1,0:T(8,128)(2,1)}), bf16[4,32,1792]{2,1,0:T(8,128)(2,1)S(1)}, u32[]{:S(2)}, u32[]{:S(2)}) %all-to-all-start.3) | async-done | bytes 458784 | tf_op jit(solution)/shard_map/all_to_all | solution.py:34
  245.8 3.0 fusion.58
  248.8 4.3 %collective-permute-start.1 = (bf16[64,4,1792]{2,1,0:T(4,128)(2,1)}, bf16[64,4,1792]{2,1,0:T(4,128)(2,1)}, u32[]{:S(2)}, u32[]{:S(2)}) collective-permute-start(bf16[64,4,1792]{2,1,0:T(4,128)(2,1)} %fusion.58), channel_id=1, source_target_pairs={{0,4},{1,5},{2,6},{3,7},{8,12},{9,13},{10,14},{11,15},{16,20},{17,... | collective-permute-start | bytes 2752520 | tf_op jit(solution)/shard_map/ppermute | solution.py:15
  255.0 16.2 %collective-permute-done.1 = bf16[64,4,1792]{2,1,0:T(4,128)(2,1)} collective-permute-done((bf16[64,4,1792]{2,1,0:T(4,128)(2,1)}, bf16[64,4,1792]{2,1,0:T(4,128)(2,1)}, u32[]{:S(2)}, u32[]{:S(2)}) %collective-permute-start.1) | collective-permute-done | bytes 917536 | tf_op jit(solution)/shard_map/ppermute | solution.py:15
  271.2 2.6 fusion.64
  273.8 1.1 fusion.270
  275.3 11.8 %all-reduce = (f32[64,24]{0,1:T(8,128)S(1)}, f32[64]{0:T(128)S(1)}, f32[64,4,4]{2,1,0:T(4,128)S(1)}) all-reduce(f32[64,24]{0,1:T(8,128)S(1)} %convolution_bitcast_fusion, f32[64]{0:T(128)S(1)} %get-tuple-element.14, f32[64,4,4]{2,1,0:T(4,128)S(1)} %fusion.270), channel_id=1, replica_groups=mesh['dp'=4,'section'=2,'expert'=4] {'dp'}, use_global_device_ids=true, to_apply=%region_96.97 | all-reduce | flops 2624 | bytes 20992 | tf_op jit(solution)/shard_map/psum | solution.py:43
  287.4 1.3 fusion.65
  290.6 3.5 all-to-all-start.4
  294.7 13.0 %all-to-all-done.4 = bf16[4,32,1792]{2,1,0:T(8,128)(2,1)S(1)} async-done(((bf16[4,32,1792]{2,1,0:T(8,128)(2,1)}), bf16[4,32,1792]{2,1,0:T(8,128)(2,1)S(1)}, u32[]{:S(2)}, u32[]{:S(2)}) %all-to-all-start.4) | async-done | bytes 458784 | tf_op jit(solution)/shard_map/all_to_all | solution.py:89
  307.6 3.5 fusion.272
  311.2 32.9 %all-reduce.11.cloned.1.call-done = f32[128,1024]{1,0:T(8,128)} async-done(((f32[128,1024]{1,0:T(8,128)}), f32[128,1024]{1,0:T(8,128)}) %all-reduce.11.cloned.1.call-update) | async-done | bytes 524304 | tf_op jit(solution)/shard_map/psum | solution.py:30
  344.1 2.2 convolution_convert_fusion
  346.4 4.6 %all-to-all-start.5 = ((bf16[4,32,1792]{2,1,0:T(8,128)(2,1)}), bf16[4,32,1792]{2,1,0:T(8,128)(2,1)S(1)}, u32[]{:S(2)}, u32[]{:S(2)}) async-start(bf16[4,32,1792]{2,1,0:T(8,128)(2,1)} %bitcast.138), calls=%async_computation.5 | async-start | bytes 917504 | tf_op jit(solution)/shard_map/all_to_all | solution.py:34
  351.3 11.8 %all-to-all-done.5 = bf16[4,32,1792]{2,1,0:T(8,128)(2,1)S(1)} async-done(((bf16[4,32,1792]{2,1,0:T(8,128)(2,1)}), bf16[4,32,1792]{2,1,0:T(8,128)(2,1)S(1)}, u32[]{:S(2)}, u32[]{:S(2)}) %all-to-all-start.5) | async-done | bytes 458784 | tf_op jit(solution)/shard_map/all_to_all | solution.py:34
  363.9 2.0 fusion.59
  365.9 3.4 select_select_fusion
  (188 shorter events, 44.8 us)
Async XLA Ops:
  6.5 95.6 %copy-start = (bf16[1,1,512,1792]{3,2,1,0:T(8,128)(2,1)S(1)}, bf16[1,1,512,1792]{3,2,1,0:T(8,128)(2,1)}, u32[]{:S(2)}) copy-start(bf16[1,1,512,1792]{3,2,1,0:T(8,128)(2,1)} %param.13) | copy-start | bytes 5505028
  8.5 1.2 copy-start.1
  8.5 16.7 %copy-start.18 = (f32[1,24]{1,0:T(1,128)S(1)}, f32[1,24]{1,0:T(1,128)}, u32[]{:S(2)}) copy-start(f32[1,24]{1,0:T(1,128)} %param.10) | copy-start | bytes 292
  25.4 0.6 copy-start.10
  26.0 0.6 copy-start.11
  33.8 0.5 copy-start.17
  38.0 1.7 copy-start.28
  38.8 1.0 copy-start.2
  40.5 24.0 %all-to-all-start = ((bf16[4,32,1792]{2,1,0:T(8,128)(2,1)}), bf16[4,32,1792]{2,1,0:T(8,128)(2,1)S(1)}, u32[]{:S(2)}, u32[]{:S(2)}) async-start(bf16[4,32,1792]{2,1,0:T(8,128)(2,1)} %bitcast.125), calls=%async_computation | async-start | bytes 917504 | tf_op jit(solution)/shard_map/all_to_all | solution.py:89
  45.4 56.8 %all-reduce.7.cloned.1.call-start = ((), (), s32[]{:S(2)}) async-start(), calls=%async_computation.6 | async-start | bytes 1048576 | tf_op jit(solution)/shard_map/psum | solution.py:30
  58.4 4.9 %copy-start.6 = (f32[64,16]{0,1:T(8,128)S(1)}, f32[64,16]{0,1:T(8,128)}, u32[]{:S(2)}) copy-start(f32[64,16]{0,1:T(8,128)} %slice_exponential_fusion.2) | copy-start | bytes 12292
  104.4 16.7 %all-to-all-start.1 = ((bf16[4,32,1792]{2,1,0:T(8,128)(2,1)}), bf16[4,32,1792]{2,1,0:T(8,128)(2,1)S(1)}, u32[]{:S(2)}, u32[]{:S(2)}) async-start(bf16[4,32,1792]{2,1,0:T(8,128)(2,1)} %bitcast.139), calls=%async_computation.1 | async-start | bytes 917504 | tf_op jit(solution)/shard_map/all_to_all | solution.py:34
  121.1 0.7 copy-start.23
  121.2 0.7 copy-start.29
  121.2 1.2 copy-start.7
  121.2 1.2 copy-start.12
  122.4 7.5 %copy-start.14 = (s32[64]{0:T(128)S(1)}, s32[64]{0:T(128)}, u32[]{:S(2)}) copy-start(s32[64]{0:T(128)} %get-tuple-element.29) | copy-start | bytes 772
  122.4 7.5 %copy-start.16 = (s32[64]{0:T(128)S(1)}, s32[64]{0:T(128)}, u32[]{:S(2)}) copy-start(s32[64]{0:T(128)} %get-tuple-element.31) | copy-start | bytes 772
  125.6 22.4 %collective-permute-start = (bf16[64,4,1792]{2,1,0:T(4,128)(2,1)}, bf16[64,4,1792]{2,1,0:T(4,128)(2,1)}, u32[]{:S(2)}, u32[]{:S(2)}) collective-permute-start(bf16[64,4,1792]{2,1,0:T(4,128)(2,1)} %fusion.57), channel_id=1, source_target_pairs={{0,4},{1,5},{2,6},{3,7},{8,12},{9,13},{10,14},{11,15},{16,20},{17,... | collective-permute-start | bytes 2752520 | tf_op jit(solution)/shard_map/ppermute | solution.py:15
  130.9 36.5 %copy-start.26 = (s32[64]{0:T(128)}, s32[64]{0:T(128)S(1)}, u32[]{:S(2)}) copy-start(s32[64]{0:T(128)S(1)} %multiply_add_fusion.4) | copy-start | bytes 772
  150.6 13.2 %copy-start.19 = (f32[1,24]{1,0:T(1,128)S(1)}, f32[1,24]{1,0:T(1,128)}, u32[]{:S(2)}) copy-start(f32[1,24]{1,0:T(1,128)} %param.10) | copy-start | bytes 292
  151.7 15.7 %copy-start.3 = (f32[1792]{0:T(1024)S(1)}, f32[1792]{0:T(1024)}, u32[]{:S(2)}) copy-start(f32[1792]{0:T(1024)} %copy-done.2) | copy-start | bytes 21508
  168.5 17.3 %all-to-all-start.2 = ((bf16[4,32,1792]{2,1,0:T(8,128)(2,1)}), bf16[4,32,1792]{2,1,0:T(8,128)(2,1)S(1)}, u32[]{:S(2)}, u32[]{:S(2)}) async-start(bf16[4,32,1792]{2,1,0:T(8,128)(2,1)} %bitcast.127), calls=%async_computation.2 | async-start | bytes 917504 | tf_op jit(solution)/shard_map/all_to_all | solution.py:89
  172.0 53.6 %all-reduce.9.cloned.1.call-start = ((), (), s32[]{:S(2)}) async-start(), calls=%async_computation.7 | async-start | bytes 1048576 | tf_op jit(solution)/shard_map/psum | solution.py:30
  173.3 11.3 %copy-start.5 = (f32[64,16]{0,1:T(8,128)S(1)}, f32[64,16]{0,1:T(8,128)}, u32[]{:S(2)}) copy-start(f32[64,16]{0,1:T(8,128)} %slice_exponential_fusion.1) | copy-start | bytes 12292
  227.8 16.7 %all-to-all-start.3 = ((bf16[4,32,1792]{2,1,0:T(8,128)(2,1)}), bf16[4,32,1792]{2,1,0:T(8,128)(2,1)S(1)}, u32[]{:S(2)}, u32[]{:S(2)}) async-start(bf16[4,32,1792]{2,1,0:T(8,128)(2,1)} %bitcast.137), calls=%async_computation.3 | async-start | bytes 917504 | tf_op jit(solution)/shard_map/all_to_all | solution.py:34
  244.5 0.7 copy-start.22
  244.5 0.7 copy-start.27
  244.5 1.2 copy-start.8
  244.5 1.3 copy-start.13
  245.8 7.3 %copy-start.9 = (s32[64,2]{1,0:T(8,128)S(1)}, s32[64,2]{1,0:T(8,128)}, u32[]{:S(2)}) copy-start(s32[64,2]{1,0:T(8,128)} %get-tuple-element.146) | copy-start | bytes 1540
  245.8 9.0 %copy-start.15 = (s32[64]{0:T(128)S(1)}, s32[64]{0:T(128)}, u32[]{:S(2)}) copy-start(s32[64]{0:T(128)} %get-tuple-element.29) | copy-start | bytes 772
  248.8 22.4 %collective-permute-start.1 = (bf16[64,4,1792]{2,1,0:T(4,128)(2,1)}, bf16[64,4,1792]{2,1,0:T(4,128)(2,1)}, u32[]{:S(2)}, u32[]{:S(2)}) collective-permute-start(bf16[64,4,1792]{2,1,0:T(4,128)(2,1)} %fusion.58), channel_id=1, source_target_pairs={{0,4},{1,5},{2,6},{3,7},{8,12},{9,13},{10,14},{11,15},{16,20},{17,... | collective-permute-start | bytes 2752520 | tf_op jit(solution)/shard_map/ppermute | solution.py:15
  255.0 34.4 %copy-start.24 = (s32[64]{0:T(128)}, s32[64]{0:T(128)S(1)}, u32[]{:S(2)}) copy-start(s32[64]{0:T(128)S(1)} %multiply_add_fusion.3) | copy-start | bytes 772
  273.8 13.3 %copy-start.20 = (f32[1,24]{1,0:T(1,128)S(1)}, f32[1,24]{1,0:T(1,128)}, u32[]{:S(2)}) copy-start(f32[1,24]{1,0:T(1,128)} %param.10) | copy-start | bytes 292
  274.9 14.6 %copy-start.4 = (f32[1792]{0:T(1024)S(1)}, f32[1792]{0:T(1024)}, u32[]{:S(2)}) copy-start(f32[1792]{0:T(1024)} %copy-done.2) | copy-start | bytes 21508
  290.6 17.1 %all-to-all-start.4 = ((bf16[4,32,1792]{2,1,0:T(8,128)(2,1)}), bf16[4,32,1792]{2,1,0:T(8,128)(2,1)S(1)}, u32[]{:S(2)}, u32[]{:S(2)}) async-start(bf16[4,32,1792]{2,1,0:T(8,128)(2,1)} %bitcast.126), calls=%async_computation.4 | async-start | bytes 917504 | tf_op jit(solution)/shard_map/all_to_all | solution.py:89
  294.0 50.1 %all-reduce.11.cloned.1.call-start = ((), (), s32[]{:S(2)}) async-start(), calls=%async_computation.8 | async-start | bytes 1048576 | tf_op jit(solution)/shard_map/psum | solution.py:30
  346.4 16.7 %all-to-all-start.5 = ((bf16[4,32,1792]{2,1,0:T(8,128)(2,1)}), bf16[4,32,1792]{2,1,0:T(8,128)(2,1)S(1)}, u32[]{:S(2)}, u32[]{:S(2)}) async-start(bf16[4,32,1792]{2,1,0:T(8,128)(2,1)} %bitcast.138), calls=%async_computation.5 | async-start | bytes 917504 | tf_op jit(solution)/shard_map/all_to_all | solution.py:34
  351.0 12.3 %copy-start.21 = (f32[64]{0:T(128)S(1)}, f32[64]{0:T(128)}, u32[]{:S(2)}) copy-start(f32[64]{0:T(128)} %get-tuple-element.26) | copy-start | bytes 772
  351.0 12.3 %copy-start.25 = (s32[64]{0:T(128)S(1)}, s32[64]{0:T(128)}, u32[]{:S(2)}) copy-start(s32[64]{0:T(128)} %copy-done.24) | copy-start | bytes 772
  363.8 2.1 copy-start.30
  363.8 2.1 copy-start.31
  363.9 2.1 copy-start.32
Sparse Core Ops, SparseCore 0:
  68.2 33.9 all-reduce.6
  189.4 36.0 all-reduce.8
  311.3 32.8 all-reduce.10
where the time goes:
time: 380 us; the launch traced here: 376 us
  waiting for transfers between devices  166 us (44%)
  other arithmetic  63.2 us (17%)
  blocking collectives  38.8 us (10%)
  matrix products  35.5 us (9%)
  starting transfers between devices  34.3 us (9%)
  local copies, waits for them, and re-layouts  23.9 us (6%)
  between operations  13.8 us (4%)
    psum x3, waiting for transfers between devices, expert_block(): summed = lax.psum(hidden_pre, 'dp')  97.7 us
    psum x3, blocking collectives, mix_layer(): lax.psum((square_part, projected, path_gram), 'dp')  38.8 us
    ppermute x2, waiting for transfers between devices, passed_along(): lax.ppermute(value, axis, [(source, source + steps) for source in range(l...  33.3 us
    div x57, other arithmetic, doubly_stochastic_project(): stream_mixer = stream_mixer / jnp.sum(stream_mixer, axis=2, keepdims=True)  33 us
    all_to_all x3, waiting for transfers between devices, expert_block(): lax.all_to_all(expert_output_rows, 'expert', split_axis=0, concat_axis=0,...  22.4 us
    all_to_all x3, starting transfers between devices, expert_block(): lax.all_to_all(expert_output_rows, 'expert', split_axis=0, concat_axis=0,...  13.8 us
    all_to_all x3, waiting for transfers between devices, mix_layer(): lax.all_to_all(outgoing, 'expert', split_axis=0, concat_axis=0, tiled=True)  13 us
    all_to_all x3, starting transfers between devices, mix_layer(): lax.all_to_all(outgoing, 'expert', split_axis=0, concat_axis=0, tiled=True)  11.8 us
  transfers between devices with their start and end apart: 11, of which 9 were waited for; matrix products, arithmetic and copies ran while one was open for 15% of the time, Pallas kernels for 0%

commit v1 on v0

--- a/solution.py
+++ b/solution.py
@@ -27,7 +27,8 @@
     slot_rows = received.reshape(sources * items, width)
     inner = down_proj.shape[0]
     hidden_pre = jnp.dot(slot_rows, gate_up, preferred_element_type=jnp.float32)
-    summed = lax.psum(hidden_pre, "dp")
+    blocks = lax.all_gather(hidden_pre, "dp")
+    summed = jnp.sum(blocks, axis=0)
     hidden = (jax.nn.silu(summed[:, :inner]) * summed[:, inner:]).astype(jnp.bfloat16)
     expert_output_rows = jnp.dot(hidden, down_proj, preferred_element_type=jnp.float32)
     expert_output_rows = expert_output_rows.astype(jnp.bfloat16).reshape(sources, items, width)

time: 380 us -> 326 us (0.86)
  other arithmetic: 63.2 us -> 21.6 us
  local copies, waits for them, and re-layouts: 23.9 us -> 10.2 us
  waiting for transfers between devices: 166 us -> 173 us
    psum x3 -> x0, waiting for transfers between devices: 97.7 us -> none  [expert_block(): summed = lax.psum(hidden_pre, 'dp')]
    all_gather x0 -> x3, waiting for transfers between devices: none -> 66.5 us  [expert_block(): blocks = lax.all_gather(hidden_pre, 'dp')]
    div x57, other arithmetic: 33 us -> 2.1 us  [doubly_stochastic_project(): stream_mixer = stream_mixer / jnp.sum(stream_mixer, axis=2, keepdims=True)]
    all_to_all x3, waiting for transfers between devices: 13 us -> 31.5 us  [mix_layer(): lax.all_to_all(outgoing, 'expert', split_axis=0, concat_axis=0, tiled=True)]
    all_to_all x3, waiting for transfers between devices: 22.4 us -> 39.3 us  [expert_block(): lax.all_to_all(expert_output_rows, 'expert', split_axis=0, concat_axis=0,...]
    reduce_sum x0 -> x3, other arithmetic: none -> 5.41 us  [expert_block(): summed = jnp.sum(blocks, axis=0)]
    unnamed x71 -> x21, local copies, waits for them, and re-layouts: 7.82 us -> 4.99 us
  transfers between devices with their start and end apart: 11 -> 11, of which waited for: 9 -> 11; matrix products, arithmetic and copies ran while one was open for 15% -> 3% of each run, Pallas kernels for 0% -> 0%
where the time goes in v1:
time: 326 us; the launch traced here: 325 us
  waiting for transfers between devices  173 us (53%)
  blocking collectives  39.8 us (12%)
  starting transfers between devices  34.3 us (11%)
  matrix products  31.8 us (10%)
  other arithmetic  21.6 us (7%)
  between operations  13.7 us (4%)
  local copies, waits for them, and re-layouts  10.2 us (3%)
    all_gather x3, waiting for transfers between devices, expert_block(): blocks = lax.all_gather(hidden_pre, 'dp')  66.5 us
    psum x3, blocking collectives, mix_layer(): lax.psum((square_part, projected, path_gram), 'dp')  39.8 us
    all_to_all x3, waiting for transfers between devices, expert_block(): lax.all_to_all(expert_output_rows, 'expert', split_axis=0, concat_axis=0,...  39.3 us
    ppermute x2, waiting for transfers between devices, passed_along(): lax.ppermute(value, axis, [(source, source + steps) for source in range(l...  35.8 us
    all_to_all x3, waiting for transfers between devices, mix_layer(): lax.all_to_all(outgoing, 'expert', split_axis=0, concat_axis=0, tiled=True)  31.5 us
    all_to_all x3, starting transfers between devices, expert_block(): lax.all_to_all(expert_output_rows, 'expert', split_axis=0, concat_axis=0,...  13.8 us
    all_to_all x3, starting transfers between devices, mix_layer(): lax.all_to_all(outgoing, 'expert', split_axis=0, concat_axis=0, tiled=True)  11.8 us
    dot_general x3, matrix products, expert_block(): hidden_pre = jnp.dot(slot_rows, gate_up, preferred_element_type=jnp.float32)  10.4 us
  transfers between devices with their start and end apart: 11, of which 11 were waited for; matrix products, arithmetic and copies ran while one was open for 3% of the time, Pallas kernels for 0%

profile of v1, /device:TPU:0, one launch (start us, length us, event | category | flops | bytes accessed | tf_op | source)
XLA Modules:
  0.0 324.7 jit_solution(3930974689896701733)
XLA Ops:
  6.5 1.6 constant_dynamic-slice_fusion.6
  8.2 0.4 fusion.60
  8.6 1.2 fusion.129
  9.8 0.4 convolution_bitcast_fusion.2
  10.1 15.1 %all-reduce.2 = (f32[64,24]{0,1:T(8,128)S(1)}, f32[64]{0:T(128)S(1)}, f32[64,4,4]{2,1,0:T(4,128)}) all-reduce(f32[64,24]{0,1:T(8,128)S(1)} %convolution_bitcast_fusion.2, f32[64]{0:T(128)S(1)} %get-tuple-element.18, f32[64,4,4]{2,1,0:T(4,128)S(1)} %fusion.129), channel_id=1, replica_groups=mesh['dp'=4,'section'=2,'expert'=4] {'dp'}, use_global_device_ids=true, to_apply=%region_0.1 | all-reduce | flops 2624 | bytes 20992 | tf_op jit(solution)/shard_map/psum | solution.py:44
  25.5 0.3 fusion.61
  25.8 1.5 fusion.265
  27.6 0.2 select_reduce_fusion.2
  27.9 0.3 convolution_convert_fusion.5
  28.2 0.8 broadcast_in_dim.81
  29.0 4.9 %all-to-all-start = ((bf16[4,32,1792]{2,1,0:T(8,128)(2,1)}), bf16[4,32,1792]{2,1,0:T(8,128)(2,1)S(1)}, u32[]{:S(2)}, u32[]{:S(2)}) async-start(bf16[4,32,1792]{2,1,0:T(8,128)(2,1)} %bitcast.131), calls=%async_computation | async-start | bytes 917504 | tf_op jit(solution)/shard_map/all_to_all | solution.py:90
  33.9 4.8 %copy.306 = bf16[224,8,2,512]{3,1,2,0:T(8,128)(2,1)} copy(bf16[224,8,2,512]{3,2,1,0:T(2,128)(2,1)} %bitcast.124) | data formatting | bytes 7340032
  38.8 7.1 %all-to-all-done = bf16[4,32,1792]{2,1,0:T(8,128)(2,1)S(1)} async-done(((bf16[4,32,1792]{2,1,0:T(8,128)(2,1)}), bf16[4,32,1792]{2,1,0:T(8,128)(2,1)S(1)}, u32[]{:S(2)}, u32[]{:S(2)}) %all-to-all-start) | async-done | bytes 458784 | tf_op jit(solution)/shard_map/all_to_all | solution.py:90
  45.9 3.5 %fusion.266 = f32[128,1024]{1,0:T(8,128)} fusion(bf16[128,1792]{1,0:T(8,128)(2,1)S(1)} %bitcast.128, bf16[1792,1024]{1,0:T(8,128)(2,1)} %bitcast.121), kind=kOutput, calls=%fused_computation.463 | convolution fusion | flops 469762048 | bytes 4653056 | tf_op jit(solution)/shard_map/dot_general | solution.py:29
  49.9 21.7 %all-gather.7.cloned.1.call-done = f32[512,1024]{1,0:T(8,128)} async-done(((f32[128,1024]{1,0:T(8,128)}), f32[512,1024]{1,0:T(8,128)}) %all-gather.7.cloned.1.call-update) | async-done | bytes 2097168 | tf_op jit(solution)/shard_map/all_gather | solution.py:30
  71.6 1.8 reduce_sum.1255
  73.5 1.2 convolution_convert_fusion.2
  74.7 4.6 %all-to-all-start.1 = ((bf16[4,32,1792]{2,1,0:T(8,128)(2,1)}), bf16[4,32,1792]{2,1,0:T(8,128)(2,1)S(1)}, u32[]{:S(2)}, u32[]{:S(2)}) async-start(bf16[4,32,1792]{2,1,0:T(8,128)(2,1)} %bitcast.145), calls=%async_computation.1 | async-start | bytes 917504 | tf_op jit(solution)/shard_map/all_to_all | solution.py:35
  79.6 13.1 %all-to-all-done.1 = bf16[4,32,1792]{2,1,0:T(8,128)(2,1)S(1)} async-done(((bf16[4,32,1792]{2,1,0:T(8,128)(2,1)}), bf16[4,32,1792]{2,1,0:T(8,128)(2,1)S(1)}, u32[]{:S(2)}, u32[]{:S(2)}) %all-to-all-start.1) | async-done | bytes 458784 | tf_op jit(solution)/shard_map/all_to_all | solution.py:35
  92.9 0.6 fusion.154
  93.5 3.2 fusion.57
  96.6 4.3 %collective-permute-start = (bf16[64,4,1792]{2,1,0:T(4,128)(2,1)}, bf16[64,4,1792]{2,1,0:T(4,128)(2,1)}, u32[]{:S(2)}, u32[]{:S(2)}) collective-permute-start(bf16[64,4,1792]{2,1,0:T(4,128)(2,1)} %fusion.57), channel_id=1, source_target_pairs={{0,4},{1,5},{2,6},{3,7},{8,12},{9,13},{10,14},{11,15},{16,20},{17,... | collective-permute-start | bytes 2752520 | tf_op jit(solution)/shard_map/ppermute | solution.py:15
  101.1 0.2 select_reduce_fusion.1
  101.3 17.9 %collective-permute-done = bf16[64,4,1792]{2,1,0:T(4,128)(2,1)} collective-permute-done((bf16[64,4,1792]{2,1,0:T(4,128)(2,1)}, bf16[64,4,1792]{2,1,0:T(4,128)(2,1)}, u32[]{:S(2)}, u32[]{:S(2)}) %collective-permute-start) | collective-permute-done | bytes 917536 | tf_op jit(solution)/shard_map/ppermute | solution.py:15
  119.2 2.6 fusion.62
  121.8 1.1 fusion.267
  122.9 0.4 convolution_bitcast_fusion.1
  123.3 12.3 %all-reduce.1 = (f32[64,24]{0,1:T(8,128)S(1)}, f32[64]{0:T(128)S(1)}, f32[64,4,4]{2,1,0:T(4,128)S(1)}) all-reduce(f32[64,24]{0,1:T(8,128)S(1)} %convolution_bitcast_fusion.1, f32[64]{0:T(128)S(1)} %get-tuple-element.16, f32[64,4,4]{2,1,0:T(4,128)S(1)} %fusion.267), channel_id=1, replica_groups=mesh['dp'=4,'section'=2,'expert'=4] {'dp'}, use_global_device_ids=true, to_apply=%region_48.49 | all-reduce | flops 2624 | bytes 20992 | tf_op jit(solution)/shard_map/psum | solution.py:44
  135.9 1.3 fusion.63
  137.2 0.6 fusion.268
  137.9 0.3 convolution_convert_fusion.4
  138.2 0.8 broadcast_in_dim.84
  139.0 3.5 %all-to-all-start.2 = ((bf16[4,32,1792]{2,1,0:T(8,128)(2,1)}), bf16[4,32,1792]{2,1,0:T(8,128)(2,1)S(1)}, u32[]{:S(2)}, u32[]{:S(2)}) async-start(bf16[4,32,1792]{2,1,0:T(8,128)(2,1)} %bitcast.132), calls=%async_computation.2 | async-start | bytes 917504 | tf_op jit(solution)/shard_map/all_to_all | solution.py:90
  142.6 12.2 %all-to-all-done.2 = bf16[4,32,1792]{2,1,0:T(8,128)(2,1)S(1)} async-done(((bf16[4,32,1792]{2,1,0:T(8,128)(2,1)}), bf16[4,32,1792]{2,1,0:T(8,128)(2,1)S(1)}, u32[]{:S(2)}, u32[]{:S(2)}) %all-to-all-start.2) | async-done | bytes 458784 | tf_op jit(solution)/shard_map/all_to_all | solution.py:90
  154.9 3.5 %fusion.269 = f32[128,1024]{1,0:T(8,128)} fusion(bf16[128,1792]{1,0:T(8,128)(2,1)S(1)} %bitcast.130, bf16[1792,1024]{1,0:T(8,128)(2,1)} %bitcast.122), kind=kOutput, calls=%fused_computation.466 | convolution fusion | flops 469762048 | bytes 4653056 | tf_op jit(solution)/shard_map/dot_general | solution.py:29
  158.9 22.4 %all-gather.9.cloned.1.call-done = f32[512,1024]{1,0:T(8,128)} async-done(((f32[128,1024]{1,0:T(8,128)}), f32[512,1024]{1,0:T(8,128)}) %all-gather.9.cloned.1.call-update) | async-done | bytes 2097168 | tf_op jit(solution)/shard_map/all_gather | solution.py:30
  181.3 1.8 reduce_sum.1299
  183.1 1.2 convolution_convert_fusion.1
  184.3 4.6 %all-to-all-start.3 = ((bf16[4,32,1792]{2,1,0:T(8,128)(2,1)}), bf16[4,32,1792]{2,1,0:T(8,128)(2,1)S(1)}, u32[]{:S(2)}, u32[]{:S(2)}) async-start(bf16[4,32,1792]{2,1,0:T(8,128)(2,1)} %bitcast.143), calls=%async_computation.3 | async-start | bytes 917504 | tf_op jit(solution)/shard_map/all_to_all | solution.py:35
  189.3 13.1 %all-to-all-done.3 = bf16[4,32,1792]{2,1,0:T(8,128)(2,1)S(1)} async-done(((bf16[4,32,1792]{2,1,0:T(8,128)(2,1)}), bf16[4,32,1792]{2,1,0:T(8,128)(2,1)S(1)}, u32[]{:S(2)}, u32[]{:S(2)}) %all-to-all-start.3) | async-done | bytes 458784 | tf_op jit(solution)/shard_map/all_to_all | solution.py:35
  202.6 0.6 fusion.152
  203.1 3.0 fusion.58
  206.1 4.3 %collective-permute-start.1 = (bf16[64,4,1792]{2,1,0:T(4,128)(2,1)}, bf16[64,4,1792]{2,1,0:T(4,128)(2,1)}, u32[]{:S(2)}, u32[]{:S(2)}) collective-permute-start(bf16[64,4,1792]{2,1,0:T(4,128)(2,1)} %fusion.58), channel_id=1, source_target_pairs={{0,4},{1,5},{2,6},{3,7},{8,12},{9,13},{10,14},{11,15},{16,20},{17,... | collective-permute-start | bytes 2752520 | tf_op jit(solution)/shard_map/ppermute | solution.py:15
  210.5 0.2 select_reduce_fusion
  210.7 17.9 %collective-permute-done.1 = bf16[64,4,1792]{2,1,0:T(4,128)(2,1)} collective-permute-done((bf16[64,4,1792]{2,1,0:T(4,128)(2,1)}, bf16[64,4,1792]{2,1,0:T(4,128)(2,1)}, u32[]{:S(2)}, u32[]{:S(2)}) %collective-permute-start.1) | collective-permute-done | bytes 917536 | tf_op jit(solution)/shard_map/ppermute | solution.py:15
  228.7 2.6 fusion.64
  231.3 1.1 fusion.270
  232.4 0.4 convolution_bitcast_fusion
  232.7 12.4 %all-reduce = (f32[64,24]{0,1:T(8,128)S(1)}, f32[64]{0:T(128)S(1)}, f32[64,4,4]{2,1,0:T(4,128)S(1)}) all-reduce(f32[64,24]{0,1:T(8,128)S(1)} %convolution_bitcast_fusion, f32[64]{0:T(128)S(1)} %get-tuple-element.14, f32[64,4,4]{2,1,0:T(4,128)S(1)} %fusion.270), channel_id=1, replica_groups=mesh['dp'=4,'section'=2,'expert'=4] {'dp'}, use_global_device_ids=true, to_apply=%region_96.97 | all-reduce | flops 2624 | bytes 20992 | tf_op jit(solution)/shard_map/psum | solution.py:44
  245.4 1.3 fusion.65
  246.7 0.6 fusion.271
  247.4 0.3 convolution_convert_fusion.3
  247.7 0.8 broadcast_in_dim.87
  248.5 3.5 %all-to-all-start.4 = ((bf16[4,32,1792]{2,1,0:T(8,128)(2,1)}), bf16[4,32,1792]{2,1,0:T(8,128)(2,1)S(1)}, u32[]{:S(2)}, u32[]{:S(2)}) async-start(bf16[4,32,1792]{2,1,0:T(8,128)(2,1)} %bitcast.133), calls=%async_computation.4 | async-start | bytes 917504 | tf_op jit(solution)/shard_map/all_to_all | solution.py:90
  252.2 12.2 %all-to-all-done.4 = bf16[4,32,1792]{2,1,0:T(8,128)(2,1)S(1)} async-done(((bf16[4,32,1792]{2,1,0:T(8,128)(2,1)}), bf16[4,32,1792]{2,1,0:T(8,128)(2,1)S(1)}, u32[]{:S(2)}, u32[]{:S(2)}) %all-to-all-start.4) | async-done | bytes 458784 | tf_op jit(solution)/shard_map/all_to_all | solution.py:90
  264.4 3.5 %fusion.272 = f32[128,1024]{1,0:T(8,128)} fusion(bf16[128,1792]{1,0:T(8,128)(2,1)S(1)} %bitcast.129, bf16[1792,1024]{1,0:T(8,128)(2,1)} %bitcast.123), kind=kOutput, calls=%fused_computation.469 | convolution fusion | flops 469762048 | bytes 4653056 | tf_op jit(solution)/shard_map/dot_general | solution.py:29
  268.5 22.4 %all-gather.11.cloned.1.call-done = f32[512,1024]{1,0:T(8,128)} async-done(((f32[128,1024]{1,0:T(8,128)}), f32[512,1024]{1,0:T(8,128)}) %all-gather.11.cloned.1.call-update) | async-done | bytes 2097168 | tf_op jit(solution)/shard_map/all_gather | solution.py:30
  290.8 1.8 reduce_sum.1343
  292.6 1.2 convolution_convert_fusion
  293.9 4.6 %all-to-all-start.5 = ((bf16[4,32,1792]{2,1,0:T(8,128)(2,1)}), bf16[4,32,1792]{2,1,0:T(8,128)(2,1)S(1)}, u32[]{:S(2)}, u32[]{:S(2)}) async-start(bf16[4,32,1792]{2,1,0:T(8,128)(2,1)} %bitcast.144), calls=%async_computation.5 | async-start | bytes 917504 | tf_op jit(solution)/shard_map/all_to_all | solution.py:35
  298.8 13.1 %all-to-all-done.5 = bf16[4,32,1792]{2,1,0:T(8,128)(2,1)S(1)} async-done(((bf16[4,32,1792]{2,1,0:T(8,128)(2,1)}), bf16[4,32,1792]{2,1,0:T(8,128)(2,1)S(1)}, u32[]{:S(2)}, u32[]{:S(2)}) %all-to-all-start.5) | async-done | bytes 458784 | tf_op jit(solution)/shard_map/all_to_all | solution.py:35
  312.1 0.6 fusion.150
  312.6 2.0 fusion.59
  314.7 3.4 %select_select_fusion = bf16[1,2,64,4,1792]{4,3,2,1,0:T(4,128)(2,1)} fusion(pred[2]{0:T(512)(128)(4,1)S(1)} %iota_compare_fusion.13, pred[2]{0:T(512)(128)(4,1)S(1)} %iota_compare_fusion.14, pred[2]{0:T(512)(128)(4,1)S(1)} %iota_compare_fusion.12, bf16[64,4,1792]{2,1,0:T(4,128)(2,1)} %fusion.57, bf16[64,4,1792]{2,1,0:T(4,128)(2,1)} %fusion.58, ...), kind=kLoop, calls=%fused_computation.84 | loop fusion | flops 2752512 | bytes 4587526 | tf_op jit(solution)/shard_map/jit(_where)/select_n | solution.py:132
  (141 shorter events, 5.2 us)
Async XLA Ops:
  6.5 66.9 %copy-start = (bf16[1,1,512,1792]{3,2,1,0:T(8,128)(2,1)S(1)}, bf16[1,1,512,1792]{3,2,1,0:T(8,128)(2,1)}, u32[]{:S(2)}) copy-start(bf16[1,1,512,1792]{3,2,1,0:T(8,128)(2,1)} %param.13) | copy-start | bytes 5505028
  8.5 1.2 copy-start.1
  8.5 16.7 %copy-start.5 = (f32[1,24]{1,0:T(1,128)S(1)}, f32[1,24]{1,0:T(1,128)}, u32[]{:S(2)}) copy-start(f32[1,24]{1,0:T(1,128)} %param.10) | copy-start | bytes 292
  9.8 17.7 %copy-start.6 = (s32[1,2,64,1]{2,3,1,0:T(1,128)S(1)}, s32[1,2,64,1]{2,3,1,0:T(1,128)}, u32[]{:S(2)}) copy-start(s32[1,2,64,1]{2,3,1,0:T(1,128)} %param.14) | copy-start | bytes 1540
  9.8 18.1 %copy-start.4 = (bf16[1,1792]{1,0:T(2,128)(2,1)S(1)}, bf16[1,1792]{1,0:T(2,128)(2,1)}, u32[]{:S(2)}) copy-start(bf16[1,1792]{1,0:T(2,128)(2,1)} %param.11) | copy-start | bytes 10756
  29.0 16.9 %all-to-all-start = ((bf16[4,32,1792]{2,1,0:T(8,128)(2,1)}), bf16[4,32,1792]{2,1,0:T(8,128)(2,1)S(1)}, u32[]{:S(2)}, u32[]{:S(2)}) async-start(bf16[4,32,1792]{2,1,0:T(8,128)(2,1)} %bitcast.131), calls=%async_computation | async-start | bytes 917504 | tf_op jit(solution)/shard_map/all_to_all | solution.py:90
  33.8 37.8 %all-gather.7.cloned.1.call-start = ((), (), s32[]{:S(2)}) async-start(), calls=%async_computation.6 | async-start | bytes 2621440 | tf_op jit(solution)/shard_map/all_gather | solution.py:30
  73.5 6.1 %copy-start.7 = (f32[1,2,64,1]{2,3,1,0:T(1,128)S(1)}, f32[1,2,64,1]{2,3,1,0:T(1,128)}, u32[]{:S(2)}) copy-start(f32[1,2,64,1]{2,3,1,0:T(1,128)} %param.15) | copy-start | bytes 1540
  74.7 18.1 %all-to-all-start.1 = ((bf16[4,32,1792]{2,1,0:T(8,128)(2,1)}), bf16[4,32,1792]{2,1,0:T(8,128)(2,1)S(1)}, u32[]{:S(2)}, u32[]{:S(2)}) async-start(bf16[4,32,1792]{2,1,0:T(8,128)(2,1)} %bitcast.145), calls=%async_computation.1 | async-start | bytes 917504 | tf_op jit(solution)/shard_map/all_to_all | solution.py:35
  96.6 22.6 %collective-permute-start = (bf16[64,4,1792]{2,1,0:T(4,128)(2,1)}, bf16[64,4,1792]{2,1,0:T(4,128)(2,1)}, u32[]{:S(2)}, u32[]{:S(2)}) collective-permute-start(bf16[64,4,1792]{2,1,0:T(4,128)(2,1)} %fusion.57), channel_id=1, source_target_pairs={{0,4},{1,5},{2,6},{3,7},{8,12},{9,13},{10,14},{11,15},{16,20},{17,... | collective-permute-start | bytes 2752520 | tf_op jit(solution)/shard_map/ppermute | solution.py:15
  121.8 1.1 copy-start.2
  139.0 15.9 %all-to-all-start.2 = ((bf16[4,32,1792]{2,1,0:T(8,128)(2,1)}), bf16[4,32,1792]{2,1,0:T(8,128)(2,1)S(1)}, u32[]{:S(2)}, u32[]{:S(2)}) async-start(bf16[4,32,1792]{2,1,0:T(8,128)(2,1)} %bitcast.132), calls=%async_computation.2 | async-start | bytes 917504 | tf_op jit(solution)/shard_map/all_to_all | solution.py:90
  142.5 38.9 %all-gather.9.cloned.1.call-start = ((), (), s32[]{:S(2)}) async-start(), calls=%async_computation.7 | async-start | bytes 2621440 | tf_op jit(solution)/shard_map/all_gather | solution.py:30
  184.3 18.1 %all-to-all-start.3 = ((bf16[4,32,1792]{2,1,0:T(8,128)(2,1)}), bf16[4,32,1792]{2,1,0:T(8,128)(2,1)S(1)}, u32[]{:S(2)}, u32[]{:S(2)}) async-start(bf16[4,32,1792]{2,1,0:T(8,128)(2,1)} %bitcast.143), calls=%async_computation.3 | async-start | bytes 917504 | tf_op jit(solution)/shard_map/all_to_all | solution.py:35
  206.1 22.6 %collective-permute-start.1 = (bf16[64,4,1792]{2,1,0:T(4,128)(2,1)}, bf16[64,4,1792]{2,1,0:T(4,128)(2,1)}, u32[]{:S(2)}, u32[]{:S(2)}) collective-permute-start(bf16[64,4,1792]{2,1,0:T(4,128)(2,1)} %fusion.58), channel_id=1, source_target_pairs={{0,4},{1,5},{2,6},{3,7},{8,12},{9,13},{10,14},{11,15},{16,20},{17,... | collective-permute-start | bytes 2752520 | tf_op jit(solution)/shard_map/ppermute | solution.py:15
  231.3 1.1 copy-start.3
  248.5 15.9 %all-to-all-start.4 = ((bf16[4,32,1792]{2,1,0:T(8,128)(2,1)}), bf16[4,32,1792]{2,1,0:T(8,128)(2,1)S(1)}, u32[]{:S(2)}, u32[]{:S(2)}) async-start(bf16[4,32,1792]{2,1,0:T(8,128)(2,1)} %bitcast.133), calls=%async_computation.4 | async-start | bytes 917504 | tf_op jit(solution)/shard_map/all_to_all | solution.py:90
  252.0 38.9 %all-gather.11.cloned.1.call-start = ((), (), s32[]{:S(2)}) async-start(), calls=%async_computation.8 | async-start | bytes 2621440 | tf_op jit(solution)/shard_map/all_gather | solution.py:30
  293.9 18.1 %all-to-all-start.5 = ((bf16[4,32,1792]{2,1,0:T(8,128)(2,1)}), bf16[4,32,1792]{2,1,0:T(8,128)(2,1)S(1)}, u32[]{:S(2)}, u32[]{:S(2)}) async-start(bf16[4,32,1792]{2,1,0:T(8,128)(2,1)} %bitcast.144), calls=%async_computation.5 | async-start | bytes 917504 | tf_op jit(solution)/shard_map/all_to_all | solution.py:35
Sparse Core Ops, SparseCore 0:
  49.5 22.0 all-gather.6
  158.5 22.7 all-gather.8
  268.0 22.7 all-gather.10
